TPU v7x, 16 devices: a whole 2x2x2 slice. The times are simulated.
16 devices in a mesh: rep: 1, dp: 16 (over x, y, z, core).
Axes of the slice: x: 2, y: 2, z: 2, core: 2. Of those that a mesh axis runs over, the one named last changes fastest.
Arguments:
- a: bfloat16 [16, 4, 4096, 1024], P(('rep', 'dp'))
- g: bfloat16 [16, 4, 4096, 3200], P(('rep', 'dp'))
Outputs:
- output: bfloat16 [4, 1024, 3200], P('rep')
All inputs are finite; a program needn't handle non-finite values.
Results may differ from a plain program's by a relative error of at most 0.012.
Values are sent between devices in bfloat16 or wider.
A program may use at most 2 GiB of HBM per device.

v0:
```python
import jax
import jax.numpy as jnp


def solution(mesh):
    groups = mesh.shape["rep"]

    def step(a, g):
        a, g = (t.reshape(groups, -1, *t.shape[1:]) for t in (a, g))
        sums = jnp.einsum("rsntd,rsntf->rndf", a, g, preferred_element_type=jnp.float32)
        return sums.astype(jnp.bfloat16).reshape(-1, *sums.shape[2:])

    return step
```

profile of v0, /device:TPU:0, one launch (start us, length us, event | category | flops | bytes accessed | tf_op | source)
XLA Modules:
  0.0 603.7 jit_solution(17367925659442142318)
XLA Ops:
  0.0 128.3 %fusion = f32[4,1024,3200]{2,1,0:T(8,128)} fusion(bf16[1,4,4096,3200]{3,2,1,0:T(8,128)(2,1)} %param.1, bf16[1,4,4096,1024]{3,2,1,0:T(8,128)(2,1)} %param), kind=kOutput, calls=%fused_computation | convolution fusion | flops 107374182400 | bytes 190840832 | tf_op jit(solution)/rsntd,rsntf->rndf/dot_general | solution.py:10
  128.3 475.4 %all-reduce.2 = bf16[4,1024,3200]{2,1,0:T(8,128)(2,1)} all-reduce(f32[4,1024,3200]{2,1,0:T(8,128)} %fusion), channel_id=1, replica_groups=mesh['axis_0'=16] {'axis_0'}, use_global_device_ids=true, to_apply=%add.clone | all-reduce | flops 13107200 | bytes 78643200 | tf_op jit(solution)/rsntd,rsntf->rndf/dot_general | solution.py:10
where the time goes:
time: 604 us
  blocking collectives  475 us (79%)
  matrix products  128 us (21%)
    dot_general x1, blocking collectives, step(): jnp.einsum('rsntd,rsntf->rndf', a, g, preferred_element_type=jnp.float32)  475 us
    dot_general x1, matrix products, step(): jnp.einsum('rsntd,rsntf->rndf', a, g, preferred_element_type=jnp.float32)  128 us

commit v1 on v0

v1 whole, which is shorter than its diff:
```python
import functools

import jax
import jax.numpy as jnp
from jax import lax
from jax.experimental import pallas as pl
from jax.experimental.pallas import tpu as pltpu
from jax.sharding import PartitionSpec as P

MESH = pl.DeviceIdType.MESH
F32 = jnp.float32
BF16 = jnp.bfloat16

N, T, D, F = 4, 4096, 1024, 3200
H = D // 2
W = 512
PER = F // W
REM = F - PER * W
CH = N * PER
NCH = CH + 1
PARTS = 4
PR = H // PARTS
TB = 512
R = 4
RA = 6
D1, D2, D3, D4, D5, D6, D7, D8 = 1, 3, 4, 5, 6, 8, 10, 12


def main_kernel(a_ref, g_ref, out_ref, aT, ast, gv, grem, acc, xacc, sb0, rb0, sb1, rb1, sb2, rb2, sb3, rb3, fb,
                ssem, rsem, asem, gsem, remsem, lsem):
    me = lax.axis_index("dp")
    core = me % 2
    other = me + 1 - 2 * core

    def stride(d):
        return 8 - 5 * d + d * d

    def bit(d):
        return (me // stride(d)) % 2

    def partner(d):
        return me + stride(d) * (1 - 2 * bit(d))

    barrier = pltpu.get_barrier_semaphore()
    for peer in (other, partner(0), partner(1), partner(2)):
        pl.semaphore_signal(barrier, inc=1, device_id={"dp": peer}, device_id_type=MESH)

    def dim(p, k, i):
        rot = p if p < 3 else k % 3
        return (rot + i) % 3

    def rows(x, m):
        return pl.multiple_of(x, m)

    def remote(src, dst, ph, r, p, peer):
        return pltpu.make_async_remote_copy(
            src_ref=src, dst_ref=dst, send_sem=ssem.at[ph, r, p], recv_sem=rsem.at[ph, r, p],
            device_id={"dp": peer}, device_id_type=MESH)

    def a_copy(n, q, slot):
        return pltpu.make_async_copy(a_ref.at[0, n, pl.ds(rows(q * TB, TB), TB), :], ast.at[slot], asem.at[slot])

    def g_copy(k):
        n, j = k // PER, k % PER
        return pltpu.make_async_copy(g_ref.at[0, n, :, pl.ds(pl.multiple_of(j * W, W), W)], gv.at[k % 2], gsem.at[k % 2])

    def rem_copy(n):
        return pltpu.make_async_copy(g_ref.at[0, n, :, pl.ds(PER * W, REM)], grem, remsem)

    def transpose(n, q, slot):
        aT[n % 2, :, pl.ds(rows(q * TB, TB), TB)] = ast[slot].T

    for q in range(2):
        a_copy(0, q, q).start()
    g_copy(0).start()

    def first(q, _):
        a_copy(0, q, q % 2).wait()
        transpose(0, q, q % 2)

        @pl.when(q + 2 < T // TB)
        def _():
            a_copy(0, q + 2, q % 2).start()
        return 0

    lax.fori_loop(0, T // TB, first, 0)
    pl.semaphore_wait(barrier, 4)

    def x0(k):
        r = k % R
        return remote(sb0.at[r], rb0.at[r], 0, r, 0, other)

    def x1(k, p):
        r = k % R
        return remote(sb1.at[r, p], rb1.at[r, p], 1, r, p, partner(dim(p, k, 0)))

    def x2(k, p):
        r = k % R
        return remote(sb2.at[r, p], rb2.at[r, p], 2, r, p, partner(dim(p, k, 1)))

    def x3(k, p):
        r = k % R
        return remote(sb3.at[r, p], rb3.at[r, p], 3, r, p, partner(dim(p, k, 2)))

    def offs(k, p):
        o1 = p * PR + bit(dim(p, k, 0)) * (PR // 2)
        o2 = o1 + bit(dim(p, k, 1)) * (PR // 4)
        o3 = o2 + bit(dim(p, k, 2)) * (PR // 8)
        return o1, o2, o3

    def block(k, o, m):
        return out_ref.at[k, pl.ds(rows(core * H + o, m), m), :]

    def own(k, p):
        return pltpu.make_async_copy(fb.at[k % R, p], block(k, offs(k, p)[2], PR // 8), lsem.at[k % R, p])

    def y1(k, p):
        return remote(fb.at[k % R, p], block(k, offs(k, p)[2], PR // 8), 4, k % R, p, partner(dim(p, k, 2)))

    def y2(k, p):
        b = block(k, offs(k, p)[1], PR // 4)
        return remote(b, b, 5, k % R, p, partner(dim(p, k, 1)))

    def y3(k, p):
        b = block(k, offs(k, p)[0], PR // 2)
        return remote(b, b, 6, k % R, p, partner(dim(p, k, 0)))

    def y4(k):
        b = block(k, 0, H)
        return remote(b, b, 7, k % R, 0, other)

    def stage1(k):
        x0(k).wait()
        r, s = k % R, k % RA
        for p in range(PARTS):
            v = bit(dim(p, k, 0))
            give = rows(p * PR + (1 - v) * (PR // 2), PR // 2)
            keep = rows(p * PR + v * (PR // 2), PR // 2)
            sb1[r, p] = (acc[s, pl.ds(give, PR // 2), :] + rb0[r, pl.ds(give, PR // 2), :].astype(F32)).astype(BF16)
            x1(k, p).start()
            acc[s, pl.ds(keep, PR // 2), :] += rb0[r, pl.ds(keep, PR // 2), :].astype(F32)

    def halve(k, i, x_in, x_out, rb, sb):
        r, s = k % R, k % RA
        m = PR // (2 * 2 ** i)
        for p in range(PARTS):
            x_in(k, p).wait()
            base = offs(k, p)[i - 1]
            v = bit(dim(p, k, i))
            give, keep = rows((1 - v) * m, m), rows(v * m, m)
            sb[r, p] = (acc[s, pl.ds(rows(base + give, m), m), :] + rb[r, p, pl.ds(give, m), :].astype(F32)).astype(BF16)
            x_out(k, p).start()
            acc[s, pl.ds(rows(base + keep, m), m), :] += rb[r, p, pl.ds(keep, m), :].astype(F32)

    def stage4(k):
        r, s = k % R, k % RA
        m = PR // 8
        for p in range(PARTS):
            x3(k, p).wait()
            o = rows(offs(k, p)[2], m)
            fb[r, p] = (acc[s, pl.ds(o, m), :] + rb3[r, p].astype(F32)).astype(BF16)
            y1(k, p).start()
            own(k, p).start()

    def stage5(k):
        for p in range(PARTS):
            own(k, p).wait()
            y1(k, p).wait()
            y2(k, p).start()

    def stage6(k):
        for p in range(PARTS):
            y2(k, p).wait()
            y3(k, p).start()

    def stage7(k):
        for p in range(PARTS):
            y3(k, p).wait()
        y4(k).start()

    def stage8(k):
        y4(k).wait()

    stages = (
        (D1, stage1),
        (D2, lambda k: halve(k, 1, x1, x2, rb1, sb2)),
        (D3, lambda k: halve(k, 2, x2, x3, rb2, sb3)),
        (D4, stage4), (D5, stage5), (D6, stage6), (D7, stage7), (D8, stage8))

    def half(u, _):
        k, h = u // 2, u % 2

        @pl.when(k < CH)
        def _():
            n, j = k // PER, k % PER
            hs = 2 * j + h

            @pl.when(h == 0)
            def _():
                g_copy(k).wait()

                @pl.when(k + 1 < CH)
                def _():
                    g_copy(k + 1).start()

            @pl.when(jnp.logical_and(hs == 0, n + 1 < N))
            def _():
                for q in range(2):
                    a_copy(n + 1, q, q).start()

            @pl.when(hs == 2 * (PER - 2))
            def _():
                rem_copy(n).start()

            slot = (1 - h) * RA + h * (k % RA)
            ro = rows((h * core + (1 - h) * (1 - core)) * H, H)
            acc[slot] = jnp.dot(aT[n % 2, pl.ds(ro, H), :], gv[k % 2], preferred_element_type=F32)

            @pl.when(jnp.logical_and(jnp.logical_and(hs >= 1, hs <= T // TB), n + 1 < N))
            def _():
                q = hs - 1
                a_copy(n + 1, q, q % 2).wait()
                transpose(n + 1, q, q % 2)

                @pl.when(q + 2 < T // TB)
                def _():
                    a_copy(n + 1, q + 2, q % 2).start()

            @pl.when(h == 0)
            def _():
                sb0[k % R] = acc[RA].astype(BF16)
                x0(k).start()

            @pl.when(j == PER - 1)
            def _():
                @pl.when(h == 0)
                def _():
                    rem_copy(n).wait()
                xacc[h, :, pl.ds(pl.multiple_of(n * REM, REM), REM)] = jnp.dot(
                    aT[n % 2, pl.ds(ro, H), :], grem[...], preferred_element_type=F32)

        @pl.when(u == 2 * CH)
        def _():
            sb0[k % R] = xacc[0].astype(BF16)
            x0(k).start()
            acc[k % RA] = xacc[1]

        for delay, stage in stages:
            w = u - delay

            @pl.when(jnp.logical_and(jnp.logical_and(w >= 0, w < 2 * NCH), (u + delay) % 2 == 0))
            def _():
                stage((u - delay) // 2)
        return 0

    lax.fori_loop(0, 2 * CH + D8 + 1, half, 0)


def place_kernel(c_ref, o_ref, buf, isem, osem):
    ins = [pltpu.make_async_copy(c_ref.at[k], buf.at[k], isem.at[k]) for k in range(NCH)]
    outs = []
    for k in range(CH):
        n, j = k // PER, k % PER
        outs.append([pltpu.make_async_copy(buf.at[k], o_ref.at[n, :, pl.ds(j * W, W)], osem.at[k])])
    outs.append([pltpu.make_async_copy(buf.at[CH, :, pl.ds(n * REM, REM)], o_ref.at[n, :, pl.ds(PER * W, REM)],
                                       osem.at[CH + n]) for n in range(N)])
    for c in ins:
        c.start()
    for c, o in zip(ins, outs):
        c.wait()
        for x in o:
            x.start()
    for o in outs:
        for x in o:
            x.wait()


def solution(mesh):
    def step(a, g):
        hbm = pl.BlockSpec(memory_space=pl.ANY)
        dma = pltpu.SemaphoreType.DMA
        chunks = pl.pallas_call(
            main_kernel,
            out_shape=jax.ShapeDtypeStruct((NCH, D, W), BF16),
            in_specs=[hbm] * 2,
            out_specs=hbm,
            scratch_shapes=[
                pltpu.VMEM((2, D, T), BF16),
                pltpu.VMEM((2, TB, D), BF16),
                pltpu.VMEM((2, T, W), BF16),
                pltpu.VMEM((T, REM), BF16),
                pltpu.VMEM((RA + 1, H, W), F32),
                pltpu.VMEM((2, H, W), F32),
                pltpu.VMEM((R, H, W), BF16),
                pltpu.VMEM((R, H, W), BF16),
                pltpu.VMEM((R, PARTS, PR // 2, W), BF16),
                pltpu.VMEM((R, PARTS, PR // 2, W), BF16),
                pltpu.VMEM((R, PARTS, PR // 4, W), BF16),
                pltpu.VMEM((R, PARTS, PR // 4, W), BF16),
                pltpu.VMEM((R, PARTS, PR // 8, W), BF16),
                pltpu.VMEM((R, PARTS, PR // 8, W), BF16),
                pltpu.VMEM((R, PARTS, PR // 8, W), BF16),
                dma((8, R, PARTS)),
                dma((8, R, PARTS)),
                dma((2,)),
                dma((2,)),
                dma,
                dma((R, PARTS)),
            ],
            compiler_params=pltpu.CompilerParams(
                collective_id=0, has_side_effects=True, vmem_limit_bytes=62 * 2**20),
            name="sum_chunks",
        )(a, g)
        return pl.pallas_call(
            place_kernel,
            out_shape=jax.ShapeDtypeStruct((N, D, F), BF16),
            in_specs=[hbm],
            out_specs=hbm,
            scratch_shapes=[pltpu.VMEM((NCH, D, W), BF16), dma((NCH,)), dma((CH + N,))],
            compiler_params=pltpu.CompilerParams(vmem_limit_bytes=40 * 2**20),
            name="place_chunks",
        )(chunks)

    return jax.shard_map(step, mesh=mesh, in_specs=(P(("rep", "dp")), P(("rep", "dp"))), out_specs=P("rep"),
                         check_vma=False)
```

time: 604 us -> 283 us (0.47)
  blocking collectives: 475 us -> 0 us
  Pallas kernels: 0 us -> 283 us
  matrix products: 128 us -> 0 us
    dot_general x1 -> x0, blocking collectives: 475 us -> none  [step(): jnp.einsum('rsntd,rsntf->rndf', a, g, preferred_element_type=jnp.float32)]
    pallas_call x0 -> x2, Pallas kernels: none -> 283 us  [the longest x1 265 us: step(): pl.pallas_call(main_kernel, out_shape=jax.ShapeDtypeStruct((NCH, D, W), B...]
    dot_general x1 -> x0, matrix products: 128 us -> none  [step(): jnp.einsum('rsntd,rsntf->rndf', a, g, preferred_element_type=jnp.float32)]
where the time goes in v1:
time: 283 us
  Pallas kernels  283 us (100%)
    pallas_call x1, Pallas kernels, step(): pl.pallas_call(main_kernel, out_shape=jax.ShapeDtypeStruct((NCH, D, W), B...  265 us
    pallas_call x1, Pallas kernels, step(): pl.pallas_call(place_kernel, out_shape=jax.ShapeDtypeStruct((N, D, F), BF...  18.2 us

profile of v1, /device:TPU:0, one launch (start us, length us, event | category | flops | bytes accessed | tf_op | source)
XLA Modules:
  0.0 283.1 jit_solution(8141649882367932841)
XLA Ops:
  0.0 264.8 %sum_chunks.1.c_ref = bf16[25,1024,512]{2,1,0:T(8,128)(2,1)} custom-call(bf16[1,4,4096,1024]{3,2,1,0:T(8,128)(2,1)} %a_ref.1, bf16[1,4,4096,3200]{3,2,1,0:T(8,128)(2,1)} %g_ref.1), custom_call_target="tpu_custom_call" | custom-call | tf_op jit(solution)/shard_map/sum_chunks/pallas_call | solution.py:282
  264.8 18.2 %place_chunks.1 = bf16[4,1024,3200]{2,1,0:T(8,128)(2,1)} custom-call(bf16[25,1024,512]{2,1,0:T(8,128)(2,1)} %sum_chunks.1.c_ref), custom_call_target="tpu_custom_call" | custom-call | tf_op jit(solution)/shard_map/place_chunks/pallas_call | solution.py:314

commit v2 on v1

v2 whole, which is shorter than its diff:
```python
import functools

import jax
import jax.numpy as jnp
from jax import lax
from jax.experimental import pallas as pl
from jax.experimental.pallas import tpu as pltpu
from jax.sharding import PartitionSpec as P

LOGICAL = pl.DeviceIdType.LOGICAL
F32 = jnp.float32
BF16 = jnp.bfloat16

N, T, D, F = 4, 4096, 1024, 3200
H = D // 2
W = 512
PER = F // W
REM = F - PER * W
CH = N * PER
NCH = CH + 1
PART = ((0, 160), (160, 160), (320, 192))
TB = 512
R = 4
RA = 8
RY = 8
D1, D2, D3, D4, D5 = 1, 3, 4, 6, 8
A, B, D6 = 7, 16, 8
END = 2 * NCH
DONE = (A * (END - 1 - D6)) // B + 1
L7, L8 = 3, 4
LAST = END + NCH - DONE + L8

for _k in range(NCH):
    _u = -(-_k * B // A) + D6 if _k < DONE else END + _k - DONE
    assert _u >= 2 * _k + D5


def shift(x, s):
    return lax.shift_right_arithmetic(x, jnp.int32(s)) if isinstance(x, jax.Array) else x >> s


def low(x, m):
    return lax.bitwise_and(x, jnp.int32(m - 1)) if isinstance(x, jax.Array) else x % m


def third(k):
    return shift(k * 43, 7)


def sixth(k):
    return shift(k * 43, 8)


def main_kernel(a_ref, g_ref, out_ref, aT, ast, gv, grem, acc, xacc, sb0, rb0, sb1, rb1, sb2, rb2, sb3, rb3, fb,
                ssem, rsem, s3sem, r3sem, s4sem, r4sem, asem, gsem, remsem, lsem):
    me = lax.axis_index("dp")
    core = me % 2
    other = me + 1 - 2 * core
    strides = (8, 4, 2)
    bits = [(me // s) % 2 for s in strides]
    peers = [me + s * (1 - 2 * v) for s, v in zip(strides, bits)]

    barrier = pltpu.get_barrier_semaphore()
    for peer in [other] + peers:
        pl.semaphore_signal(barrier, inc=1, device_id=peer, device_id_type=LOGICAL)

    def at(q, v):
        return v[0] + q * (v[1] - v[0]) + shift(q * (q - 1), 1) * (v[2] - 2 * v[1] + v[0])

    def turn(k):
        q = k - 3 * third(k)
        return ([at(q, peers[e:] + peers[:e]) for e in range(3)], [at(q, bits[e:] + bits[:e]) for e in range(3)])

    def rows(x, m):
        return pl.multiple_of(x, m)

    def lanes(x):
        return pl.multiple_of(x, 128)

    def send(src, dst, send_sem, recv_sem, peer):
        return pltpu.make_async_remote_copy(
            src_ref=src, dst_ref=dst, send_sem=send_sem, recv_sem=recv_sem, device_id=peer, device_id_type=LOGICAL)

    def a_copy(n, q, slot):
        return pltpu.make_async_copy(a_ref.at[0, n, pl.ds(rows(q * TB, TB), TB), :], ast.at[slot], asem.at[slot])

    def g_copy(k):
        n = sixth(k)
        j = k - PER * n
        s = low(k, 2)
        return pltpu.make_async_copy(g_ref.at[0, n, :, pl.ds(lanes(j * W), W)], gv.at[s], gsem.at[s])

    def rem_copy(n):
        return pltpu.make_async_copy(g_ref.at[0, n, :, pl.ds(PER * W, REM)], grem, remsem)

    def transpose(n, q, slot):
        aT[low(n, 2), :, pl.ds(rows(q * TB, TB), TB)] = ast[slot].T

    for q in range(2):
        a_copy(0, q, q).start()
    g_copy(0).start()

    def first(q, _):
        a_copy(0, q, low(q, 2)).wait()
        transpose(0, q, low(q, 2))

        @pl.when(q + 2 < T // TB)
        def _():
            a_copy(0, q + 2, low(q, 2)).start()
        return 0

    lax.fori_loop(0, T // TB, first, 0)
    pl.semaphore_wait(barrier, 4)

    def x0(k):
        r = low(k, R)
        return send(sb0.at[r], rb0.at[r], ssem.at[0, r], rsem.at[0, r], other)

    def y4(k):
        b = out_ref.at[k, pl.ds(rows(core * H, H), H), :]
        y = low(k, RY)
        return send(b, b, s4sem.at[y], r4sem.at[y], other)

    def wait_parts(ref, ssem, rsem):
        c = send(ref, ref, ssem, rsem, other)
        c.wait_send()
        c.wait_recv()

    def place(k, o, m, c, w):
        return out_ref.at[k, pl.ds(rows(core * H + o, 16), m), pl.ds(lanes(c), w)]

    def stage1(k):
        x0(k).wait()
        r, s = low(k, R), low(k, RA)
        peer, bit = turn(k)
        for p, (o, m) in enumerate(PART):
            v = bit[p]
            part = pl.ds(o, m)
            give, keep = (pl.ds(lanes(c * (W // 2)), W // 2) for c in (1 - v, v))
            sb1[r, part, :] = (acc[s, part, give] + rb0[r, part, give].astype(F32)).astype(BF16)
            send(sb1.at[r, part], rb1.at[r, part], ssem.at[1, r], rsem.at[1, r], peer[p]).start()
            acc[s, part, keep] += rb0[r, part, keep].astype(F32)

    def stage2(k):
        r, s = low(k, R), low(k, RA)
        peer, bit = turn(k)
        wait_parts(sb1.at[r], ssem.at[1, r], rsem.at[1, r])
        for p, (o, m) in enumerate(PART):
            c1, v = bit[p] * (W // 2), bit[(p + 1) % 3]
            part = pl.ds(o, m)
            give, keep = (pl.ds(lanes(c * (W // 4)), W // 4) for c in (1 - v, v))
            agive, akeep = (pl.ds(lanes(c1 + c * (W // 4)), W // 4) for c in (1 - v, v))
            sb2[r, part, :] = (acc[s, part, agive] + rb1[r, part, give].astype(F32)).astype(BF16)
            send(sb2.at[r, part], rb2.at[r, part], ssem.at[2, r], rsem.at[2, r], peer[(p + 1) % 3]).start()
            acc[s, part, akeep] += rb1[r, part, keep].astype(F32)

    def stage3(k):
        r, s = low(k, R), low(k, RA)
        peer, bit = turn(k)
        wait_parts(sb2.at[r], ssem.at[2, r], rsem.at[2, r])
        for p, (o, m) in enumerate(PART):
            part = pl.ds(o, m)
            cols = pl.ds(lanes(bit[p] * (W // 2) + bit[(p + 1) % 3] * (W // 4)), W // 4)
            sb3[r, part, :] = (acc[s, part, cols] + rb2[r, part, :].astype(F32)).astype(BF16)
            send(sb3.at[r, part], rb3.at[r, part], ssem.at[3, r], rsem.at[3, r], peer[(p + 2) % 3]).start()

    def stage4(k):
        r = low(k, R)
        peer, bit = turn(k)
        wait_parts(sb3.at[r], ssem.at[3, r], rsem.at[3, r])
        for p, (o, m) in enumerate(PART):
            part = pl.ds(o, m)
            fb[r, part, :] = (sb3[r, part, :].astype(F32) + rb3[r, part, :].astype(F32)).astype(BF16)
            b = place(k, o, m, bit[p] * (W // 2) + bit[(p + 1) % 3] * (W // 4), W // 4)
            send(fb.at[r, part], b, ssem.at[4, r], rsem.at[4, r], peer[(p + 1) % 3]).start()
            pltpu.make_async_copy(fb.at[r, part], b, lsem.at[r]).start()

    def stage5(k):
        r = low(k, R)
        pltpu.make_async_copy(fb.at[r], fb.at[r], lsem.at[r]).wait()
        wait_parts(sb3.at[r], ssem.at[4, r], rsem.at[4, r])

    def stage6(k):
        y = low(k, RY)
        peer, bit = turn(k)
        for p, (o, m) in enumerate(PART):
            b = place(k, o, m, bit[p] * (W // 2), W // 2)
            send(b, b, s3sem.at[y], r3sem.at[y], peer[p]).start()

    def stage7(k):
        y = low(k, RY)
        wait_parts(sb1.at[0], s3sem.at[y], r3sem.at[y])
        y4(k).start()

    def stage8(k):
        y4(k).wait()

    stages = ((D2, stage2), (D3, stage3), (D4, stage4), (D1, stage1), (D5, stage5))
    slower = ((0, stage6), (L7, stage7), (L8, stage8))

    def half(u, _):
        k, h = shift(u, 1), low(u, 2)

        @pl.when(k < CH)
        def _():
            n = sixth(k)
            j = k - PER * n
            hs = 2 * j + h
            gs, ns = low(k, 2), low(n, 2)

            @pl.when(h == 0)
            def _():
                g_copy(k).wait()

                @pl.when(k + 1 < CH)
                def _():
                    g_copy(k + 1).start()

            @pl.when(jnp.logical_and(hs == 0, n + 1 < N))
            def _():
                for q in range(2):
                    a_copy(n + 1, q, q).start()

            @pl.when(hs == 2 * (PER - 2))
            def _():
                rem_copy(n).start()

            slot = (1 - h) * RA + h * low(k, RA)
            ro = rows((h * core + (1 - h) * (1 - core)) * H, H)
            acc[slot] = jnp.dot(aT[ns, pl.ds(ro, H), :], gv[gs], preferred_element_type=F32)

            @pl.when(jnp.logical_and(jnp.logical_and(hs >= 1, hs <= T // TB), n + 1 < N))
            def _():
                q = hs - 1
                qs = low(q, 2)
                a_copy(n + 1, q, qs).wait()
                transpose(n + 1, q, qs)

                @pl.when(q + 2 < T // TB)
                def _():
                    a_copy(n + 1, q + 2, qs).start()

            @pl.when(h == 0)
            def _():
                sb0[low(k, R)] = acc[RA].astype(BF16)
                x0(k).start()

            @pl.when(j == PER - 1)
            def _():
                @pl.when(h == 0)
                def _():
                    rem_copy(n).wait()
                xacc[h, :, pl.ds(lanes(n * REM), REM)] = jnp.dot(
                    aT[ns, pl.ds(ro, H), :], grem[...], preferred_element_type=F32)

        @pl.when(u == 2 * CH)
        def _():
            sb0[low(k, R)] = xacc[0].astype(BF16)
            x0(k).start()
            acc[low(k, RA)] = xacc[1]

        for delay, stage in stages:
            w = u - delay

            @pl.when(jnp.logical_and(jnp.logical_and(w >= 0, w < 2 * NCH), low(w, 2) == 0))
            def _():
                stage(shift(w, 1))
        for lag, stage in slower:
            v = u - lag
            w = A * (v - D6)
            early = jnp.logical_and(v < END, jnp.logical_and(w >= 0, low(w, B) < A))
            late = jnp.logical_and(v >= END, v < END + NCH - DONE)

            @pl.when(jnp.logical_or(early, late))
            def _():
                over = jnp.maximum(v - END + 1, 0)
                stage(jnp.where(over > 0, DONE - 1 + over, shift(w, 4)))
        return 0

    lax.fori_loop(0, LAST, half, 0)


def place_kernel(c_ref, o_ref, buf, isem, osem):
    ins = [pltpu.make_async_copy(c_ref.at[k], buf.at[k], isem.at[k]) for k in range(NCH)]
    outs = []
    for k in range(CH):
        n, j = k // PER, k % PER
        outs.append([pltpu.make_async_copy(buf.at[k], o_ref.at[n, :, pl.ds(j * W, W)], osem.at[k])])
    outs.append([pltpu.make_async_copy(buf.at[CH, :, pl.ds(n * REM, REM)], o_ref.at[n, :, pl.ds(PER * W, REM)],
                                       osem.at[CH + n]) for n in range(N)])
    for c in ins:
        c.start()
    for c, o in zip(ins, outs):
        c.wait()
        for x in o:
            x.start()
    for o in outs:
        for x in o:
            x.wait()


def solution(mesh):
    def step(a, g):
        hbm = pl.BlockSpec(memory_space=pl.ANY)
        dma = pltpu.SemaphoreType.DMA
        chunks = pl.pallas_call(
            main_kernel,
            out_shape=jax.ShapeDtypeStruct((NCH, D, W), BF16),
            in_specs=[hbm] * 2,
            out_specs=hbm,
            scratch_shapes=[
                pltpu.VMEM((2, D, T), BF16),
                pltpu.VMEM((2, TB, D), BF16),
                pltpu.VMEM((2, T, W), BF16),
                pltpu.VMEM((T, REM), BF16),
                pltpu.VMEM((RA + 1, H, W), F32),
                pltpu.VMEM((2, H, W), F32),
                pltpu.VMEM((R, H, W), BF16),
                pltpu.VMEM((R, H, W), BF16),
                pltpu.VMEM((R, H, W // 2), BF16),
                pltpu.VMEM((R, H, W // 2), BF16),
                pltpu.VMEM((R, H, W // 4), BF16),
                pltpu.VMEM((R, H, W // 4), BF16),
                pltpu.VMEM((R, H, W // 4), BF16),
                pltpu.VMEM((R, H, W // 4), BF16),
                pltpu.VMEM((R, H, W // 4), BF16),
                dma((5, R)),
                dma((5, R)),
                dma((RY,)),
                dma((RY,)),
                dma((RY,)),
                dma((RY,)),
                dma((2,)),
                dma((2,)),
                dma,
                dma((R,)),
            ],
            compiler_params=pltpu.CompilerParams(
                collective_id=0, has_side_effects=True, vmem_limit_bytes=62 * 2**20),
            name="sum_chunks",
        )(a, g)
        return pl.pallas_call(
            place_kernel,
            out_shape=jax.ShapeDtypeStruct((N, D, F), BF16),
            in_specs=[hbm],
            out_specs=hbm,
            scratch_shapes=[pltpu.VMEM((NCH, D, W), BF16), dma((NCH,)), dma((CH + N,))],
            compiler_params=pltpu.CompilerParams(vmem_limit_bytes=40 * 2**20),
            name="place_chunks",
        )(chunks)

    return jax.shard_map(step, mesh=mesh, in_specs=(P(("rep", "dp")), P(("rep", "dp"))), out_specs=P("rep"),
                         check_vma=False)
```

time: 283 us -> 218 us (0.77)
  Pallas kernels: 283 us -> 218 us
    pallas_call x1, Pallas kernels: 265 us -> 200 us  [step(): pl.pallas_call(main_kernel, out_shape=jax.ShapeDtypeStruct((NCH, D, W), B...]
where the time goes in v2:
time: 218 us
  Pallas kernels  218 us (100%)
    pallas_call x1, Pallas kernels, step(): pl.pallas_call(main_kernel, out_shape=jax.ShapeDtypeStruct((NCH, D, W), B...  200 us
    pallas_call x1, Pallas kernels, step(): pl.pallas_call(place_kernel, out_shape=jax.ShapeDtypeStruct((N, D, F), BF...  18.2 us

profile of v2, /device:TPU:0, one launch (start us, length us, event | category | flops | bytes accessed | tf_op | source)
XLA Modules:
  0.0 218.0 jit_solution(15347266000381622535)
XLA Ops:
  0.0 199.7 %sum_chunks.1.c_ref = bf16[25,1024,512]{2,1,0:T(8,128)(2,1)} custom-call(bf16[1,4,4096,1024]{3,2,1,0:T(8,128)(2,1)} %a_ref.1, bf16[1,4,4096,3200]{3,2,1,0:T(8,128)(2,1)} %g_ref.1), custom_call_target="tpu_custom_call" | custom-call | tf_op jit(solution)/shard_map/sum_chunks/pallas_call | solution.py:306
  199.7 18.2 %place_chunks.1 = bf16[4,1024,3200]{2,1,0:T(8,128)(2,1)} custom-call(bf16[25,1024,512]{2,1,0:T(8,128)(2,1)} %sum_chunks.1.c_ref), custom_call_target="tpu_custom_call" | custom-call | tf_op jit(solution)/shard_map/place_chunks/pallas_call | solution.py:342

commit v3 on v2

--- a/solution.py
+++ b/solution.py
@@ -23,11 +23,11 @@
 R = 4
 RA = 8
 RY = 8
-D1, D2, D3, D4, D5 = 1, 3, 4, 6, 8
-A, B, D6 = 7, 16, 8
-END = 2 * NCH
+D1, D2, D3, D4, D5 = 1, 3, 6, 8, 10
+A, B, D6 = 8, 16, 10
+END = 2 * NCH + 10
 DONE = (A * (END - 1 - D6)) // B + 1
-L7, L8 = 3, 4
+L7, L8 = 4, 5
 LAST = END + NCH - DONE + L8
 
 for _k in range(NCH):
@@ -96,17 +96,17 @@
     def transpose(n, q, slot):
         aT[low(n, 2), :, pl.ds(rows(q * TB, TB), TB)] = ast[slot].T
 
-    for q in range(2):
+    for q in range(4):
         a_copy(0, q, q).start()
     g_copy(0).start()
 
     def first(q, _):
-        a_copy(0, q, low(q, 2)).wait()
-        transpose(0, q, low(q, 2))
-
-        @pl.when(q + 2 < T // TB)
+        a_copy(0, q, low(q, 4)).wait()
+        transpose(0, q, low(q, 4))
+
+        @pl.when(q + 4 < T // TB)
         def _():
-            a_copy(0, q + 2, low(q, 2)).start()
+            a_copy(0, q + 4, low(q, 4)).start()
         return 0
 
     lax.fori_loop(0, T // TB, first, 0)
@@ -310,7 +310,7 @@
             out_specs=hbm,
             scratch_shapes=[
                 pltpu.VMEM((2, D, T), BF16),
-                pltpu.VMEM((2, TB, D), BF16),
+                pltpu.VMEM((4, TB, D), BF16),
                 pltpu.VMEM((2, T, W), BF16),
                 pltpu.VMEM((T, REM), BF16),
                 pltpu.VMEM((RA + 1, H, W), F32),
@@ -330,7 +330,7 @@
                 dma((RY,)),
                 dma((RY,)),
                 dma((RY,)),
-                dma((2,)),
+                dma((4,)),
                 dma((2,)),
                 dma,
                 dma((R,)),

time: 218 us -> 212 us (0.972)
  Pallas kernels: 218 us -> 212 us
    pallas_call x1, Pallas kernels: 200 us -> 194 us  [step(): pl.pallas_call(main_kernel, out_shape=jax.ShapeDtypeStruct((NCH, D, W), B...]
where the time goes in v3:
time: 212 us
  Pallas kernels  212 us (100%)
    pallas_call x1, Pallas kernels, step(): pl.pallas_call(main_kernel, out_shape=jax.ShapeDtypeStruct((NCH, D, W), B...  194 us
    pallas_call x1, Pallas kernels, step(): pl.pallas_call(place_kernel, out_shape=jax.ShapeDtypeStruct((N, D, F), BF...  18.2 us

profile of v3, /device:TPU:0, one launch (start us, length us, event | category | flops | bytes accessed | tf_op | source)
XLA Modules:
  0.0 212.0 jit_solution(2359183617076081627)
XLA Ops:
  0.0 193.8 %sum_chunks.1.c_ref = bf16[25,1024,512]{2,1,0:T(8,128)(2,1)} custom-call(bf16[1,4,4096,1024]{3,2,1,0:T(8,128)(2,1)} %a_ref.1, bf16[1,4,4096,3200]{3,2,1,0:T(8,128)(2,1)} %g_ref.1), custom_call_target="tpu_custom_call" | custom-call | tf_op jit(solution)/shard_map/sum_chunks/pallas_call | solution.py:306
  193.8 18.2 %place_chunks.1 = bf16[4,1024,3200]{2,1,0:T(8,128)(2,1)} custom-call(bf16[25,1024,512]{2,1,0:T(8,128)(2,1)} %sum_chunks.1.c_ref), custom_call_target="tpu_custom_call" | custom-call | tf_op jit(solution)/shard_map/place_chunks/pallas_call | solution.py:342

commit v4 on v3

--- a/solution.py
+++ b/solution.py
@@ -285,18 +285,16 @@
     outs = []
     for k in range(CH):
         n, j = k // PER, k % PER
-        outs.append([pltpu.make_async_copy(buf.at[k], o_ref.at[n, :, pl.ds(j * W, W)], osem.at[k])])
+        outs.append([pltpu.make_async_copy(buf.at[k], o_ref.at[n, :, pl.ds(j * W, W)], osem)])
     outs.append([pltpu.make_async_copy(buf.at[CH, :, pl.ds(n * REM, REM)], o_ref.at[n, :, pl.ds(PER * W, REM)],
-                                       osem.at[CH + n]) for n in range(N)])
+                                       osem) for n in range(N)])
     for c in ins:
         c.start()
     for c, o in zip(ins, outs):
         c.wait()
         for x in o:
             x.start()
-    for o in outs:
-        for x in o:
-            x.wait()
+    pltpu.make_async_copy(o_ref, o_ref, osem).wait()
 
 
 def solution(mesh):
@@ -344,7 +342,7 @@
             out_shape=jax.ShapeDtypeStruct((N, D, F), BF16),
             in_specs=[hbm],
             out_specs=hbm,
-            scratch_shapes=[pltpu.VMEM((NCH, D, W), BF16), dma((NCH,)), dma((CH + N,))],
+            scratch_shapes=[pltpu.VMEM((NCH, D, W), BF16), dma((NCH,)), dma],
             compiler_params=pltpu.CompilerParams(vmem_limit_bytes=40 * 2**20),
             name="place_chunks",
         )(chunks)

time: 212 us -> 212 us (level)
  no operation moved by 1% of the time
where the time goes in v4:
time: 212 us
  Pallas kernels  212 us (100%)
    pallas_call x1, Pallas kernels, step(): pl.pallas_call(main_kernel, out_shape=jax.ShapeDtypeStruct((NCH, D, W), B...  194 us
    pallas_call x1, Pallas kernels, step(): pl.pallas_call(place_kernel, out_shape=jax.ShapeDtypeStruct((N, D, F), BF...  18 us

profile of v4, /device:TPU:0, one launch (start us, length us, event | category | flops | bytes accessed | tf_op | source)
XLA Modules:
  0.0 211.8 jit_solution(399072836381126388)
XLA Ops:
  0.0 193.8 %sum_chunks.1.c_ref = bf16[25,1024,512]{2,1,0:T(8,128)(2,1)} custom-call(bf16[1,4,4096,1024]{3,2,1,0:T(8,128)(2,1)} %a_ref.1, bf16[1,4,4096,3200]{3,2,1,0:T(8,128)(2,1)} %g_ref.1), custom_call_target="tpu_custom_call" | custom-call | tf_op jit(solution)/shard_map/sum_chunks/pallas_call | solution.py:304
  193.8 18.0 %place_chunks.1 = bf16[4,1024,3200]{2,1,0:T(8,128)(2,1)} custom-call(bf16[25,1024,512]{2,1,0:T(8,128)(2,1)} %sum_chunks.1.c_ref), custom_call_target="tpu_custom_call" | custom-call | tf_op jit(solution)/shard_map/place_chunks/pallas_call | solution.py:340
